TPU v7x, 32 devices: a whole 2x2x4 slice. The times are simulated.
32 devices in a mesh: snap: 2 (over x), node: 16 (over z, y, core).
Axes of the slice: x: 2, y: 2, z: 4, core: 2. Of those that a mesh axis runs over, the one named last changes fastest.
Arguments:
- features: bfloat16 [2, 16384, 512], P('snap', 'node'), may hold values from -6 to 6
- tile_rows: int32 [2, 448], P('snap', 'node'), may hold values from 0 to 127, as said below
- tile_cols: int32 [2, 448], P('snap', 'node'), may hold values from 0 to 127, as said below
- tile_values: bfloat16 [2, 448, 128, 128], P('snap', 'node'), may hold values from -0.125 to 0.125
- tile_count: int32 [2, 16], P('snap', 'node'), may hold values from 9 to 28, as said below
- w_graph: bfloat16 [512, 512], replicated, may hold values from -0.25 to 0.25
- norm_gain: float32 [512], replicated, may hold values from 0.5 to 1.5
- w_query: bfloat16 [512, 512], replicated
- w_key: bfloat16 [512, 512], replicated, may hold values from -0.25 to 0.25
- w_value: bfloat16 [512, 512], replicated, may hold values from -0.25 to 0.25
- w_out: bfloat16 [512, 512], replicated, may hold values from -0.25 to 0.25
Outputs:
- layer_out: bfloat16 [2, 16384, 512], P(None, ('node', 'snap'))
Inputs may be any that keep to these rules, and one draw needn't show every extreme that they name: `tile_rows`: every slot held by node index j (slots j * 28 to (j + 1) * 28 - 1) names a row block of that index's own nodes. `tile_cols`: every slot held by node index j names a column block of the nodes held by node indices j - 2 to j + 2. Of each node index's slots, the first tile_count are live and the rest are ignored; in each snapshot some node index has all 28 live.
All inputs are finite; a program needn't handle non-finite values.
Results may differ from a plain program's by a relative error of at most 0.0086.
Values may be sent and summed in bfloat16 or wider, within the bound.
No kernel may reach another device: no remote copies, remote signals or barrier semaphores. Data moves between devices by JAX's collectives and lax.ppermute only.
A program may use at most 64 MiB of HBM per device.

v0:
```python
import jax
import jax.numpy as jnp
from jax import lax
from jax.sharding import PartitionSpec as P

HEADS = 8
HEAD_DIM = 64


def from_behind(block, axis, distance):
    devices = range(lax.axis_size(axis))
    route = [(i - distance, i) for i in devices if i - distance in devices]
    return lax.ppermute(block, axis, route)


def norm_rows(hidden, norm_gain):
    value = hidden.astype(jnp.float32)
    mean = jnp.mean(value, axis=-1, keepdims=True)
    centred = value - mean
    variance = jnp.mean(centred * centred, axis=-1, keepdims=True)
    return (centred * lax.rsqrt(variance + 1e-05) * norm_gain).astype(jnp.bfloat16)


def project_all(normed, w_query, w_key, w_value):
    query = jnp.dot(normed, w_query, preferred_element_type=jnp.float32).astype(jnp.bfloat16)
    key = jnp.dot(normed, w_key, preferred_element_type=jnp.float32).astype(jnp.bfloat16)
    value = jnp.dot(normed, w_value, preferred_element_type=jnp.float32).astype(jnp.bfloat16)
    return (query, key, value)


def near_one(feats, offset):
    return from_behind(feats, "node", offset)


def relay_one(received, offset):
    return from_behind(received, "node", offset)


def local(
    features,
    tile_rows,
    tile_cols,
    tile_values,
    tile_count,
    w_graph,
    norm_gain,
    w_query,
    w_key,
    w_value,
    w_out,
):
    feats = features[0]
    nodes_dev, width = feats.shape
    tile = tile_values.shape[-1]
    blocks_dev = nodes_dev // tile
    here = lax.axis_index("node")
    lower = near_one(feats, 1)
    upper = near_one(feats, -1)
    window = jnp.concatenate([relay_one(lower, 1), lower, feats, upper, relay_one(upper, -1)], 0)
    window = window.reshape(5 * blocks_dev, tile, width)
    local_cols = tile_cols[0] - (here - 2) * blocks_dev
    picked = jnp.take(window, local_cols, axis=0)
    live = jnp.arange(tile_values.shape[1]) < tile_count[0, 0]
    masked = tile_values[0] * live[:, None, None].astype(jnp.bfloat16)
    prod = jnp.einsum("tij,tjd->tid", masked, picked, preferred_element_type=jnp.float32)
    local_rows = tile_rows[0] - here * blocks_dev
    select = (local_rows[None, :] == jnp.arange(blocks_dev)[:, None]).astype(jnp.float32)
    summed = jnp.einsum("bt,tid->bid", select, prod, precision=lax.Precision.HIGHEST)
    aggregated = summed.reshape(nodes_dev, width).astype(jnp.bfloat16)
    mixed = jnp.dot(aggregated, w_graph, preferred_element_type=jnp.float32)
    hidden = (feats.astype(jnp.float32) + jax.nn.relu(mixed)).astype(jnp.bfloat16)
    resident = lax.all_to_all(hidden[None], "snap", split_axis=1, concat_axis=0, tiled=True)
    snaps, nodes_here = (resident.shape[0], resident.shape[1])
    normed = norm_rows(resident, norm_gain).reshape(snaps * nodes_here, width)
    query, key, value = project_all(normed, w_query, w_key, w_value)
    query = query.reshape(snaps, nodes_here, HEADS, HEAD_DIM)
    key = key.reshape(snaps, nodes_here, HEADS, HEAD_DIM)
    value = value.reshape(snaps, nodes_here, HEADS, HEAD_DIM)
    scores = jnp.einsum(
        "snhd,unhd->nhsu", query, key, preferred_element_type=jnp.float32
    ) * HEAD_DIM ** (-0.5)
    later = jnp.arange(snaps)[:, None] >= jnp.arange(snaps)[None, :]
    scores = jnp.where(later, scores, jnp.float32(-1e30))
    weights = jax.nn.softmax(scores, axis=-1).astype(jnp.bfloat16)
    context = jnp.einsum("nhsu,unhd->snhd", weights, value, preferred_element_type=jnp.float32)
    context = context.astype(jnp.bfloat16).reshape(snaps * nodes_here, width)
    projected = jnp.dot(context, w_out, preferred_element_type=jnp.float32)
    result = resident.reshape(snaps * nodes_here, width).astype(jnp.float32) + projected
    return result.astype(jnp.bfloat16).reshape(snaps, nodes_here, width)


def solution(mesh):
    in_specs = (
        P("snap", "node", None),
        P("snap", "node"),
        P("snap", "node"),
        P("snap", "node", None, None),
        P("snap", "node"),
        P(),
        P(),
        P(),
        P(),
        P(),
        P(),
    )
    out_specs = P(None, ("node", "snap"), None)
    return jax.shard_map(local, mesh=mesh, in_specs=in_specs, out_specs=out_specs, check_vma=False)
```

profile of v0, /device:TPU:12, one launch (start us, length us, event | category | flops | bytes accessed | tf_op | source)
XLA Modules:
  0.0 149.0 jit_solution(10116249858217024973)
XLA Ops:
  0.0 2.0 %collective-permute-start = (bf16[1024,512]{1,0:T(8,128)(2,1)}, bf16[1024,512]{1,0:T(8,128)(2,1)}, u32[]{:S(2)}, u32[]{:S(2)}) collective-permute-start(bf16[1024,512]{1,0:T(8,128)(2,1)} %bitcast.63), channel_id=1, source_target_pairs={{0,1},{1,2},{2,3},{3,4},{4,5},{5,6},{6,7},{7,8},{8,9},{9,10},{10,1... | collective-permute-start | bytes 3145736 | tf_op jit(solution)/shard_map/ppermute | solution.py:13
  2.1 3.6 %collective-permute-start.2 = (bf16[1024,512]{1,0:T(8,128)(2,1)}, bf16[1024,512]{1,0:T(8,128)(2,1)S(1)}, u32[]{:S(2)}, u32[]{:S(2)}) collective-permute-start(bf16[1024,512]{1,0:T(8,128)(2,1)} %bitcast.64), channel_id=1, source_target_pairs={{1,0},{2,1},{3,2},{4,3},{5,4},{6,5},{7,6},{8,7},{9,8},{10,9},{11,1... | collective-permute-start | bytes 3145736 | tf_op jit(solution)/shard_map/ppermute | solution.py:13
  5.7 22.1 %collective-permute-done = bf16[1024,512]{1,0:T(8,128)(2,1)} collective-permute-done((bf16[1024,512]{1,0:T(8,128)(2,1)}, bf16[1024,512]{1,0:T(8,128)(2,1)}, u32[]{:S(2)}, u32[]{:S(2)}) %collective-permute-start) | collective-permute-done | bytes 1048608 | tf_op jit(solution)/shard_map/ppermute | solution.py:13
  30.4 7.6 %collective-permute-done.2 = bf16[1024,512]{1,0:T(8,128)(2,1)S(1)} collective-permute-done((bf16[1024,512]{1,0:T(8,128)(2,1)}, bf16[1024,512]{1,0:T(8,128)(2,1)S(1)}, u32[]{:S(2)}, u32[]{:S(2)}) %collective-permute-start.2) | collective-permute-done | bytes 1048608 | tf_op jit(solution)/shard_map/ppermute | solution.py:13
  38.0 3.7 %collective-permute-start.3 = (bf16[1024,512]{1,0:T(8,128)(2,1)S(1)}, bf16[1024,512]{1,0:T(8,128)(2,1)S(1)}, u32[]{:S(2)}, u32[]{:S(2)}) collective-permute-start(bf16[1024,512]{1,0:T(8,128)(2,1)S(1)} %collective-permute-done.2), channel_id=1, source_target_pairs={{1,0},{2,1},{3,2},{4,3},{5,4},{6,5},{7,6},{8,7},{9,8},{10,9},{11,1... | collective-permute-start | bytes 3145736 | tf_op jit(solution)/shard_map/ppermute | solution.py:13
  43.7 11.8 %collective-permute-done.1 = bf16[1024,512]{1,0:T(8,128)(2,1)} collective-permute-done((bf16[1024,512]{1,0:T(8,128)(2,1)}, bf16[1024,512]{1,0:T(8,128)(2,1)}, u32[]{:S(2)}, u32[]{:S(2)}) %collective-permute-start.1) | collective-permute-done | bytes 1048608 | tf_op jit(solution)/shard_map/ppermute | solution.py:13
  55.5 2.3 %constant_dynamic-update-slice_fusion.4 = bf16[5120,512]{1,0:T(8,128)(2,1)} fusion(bf16[1024,512]{1,0:T(8,128)(2,1)} %collective-permute-done.1), kind=kLoop, calls=%fused_computation.41 | loop fusion | bytes 2097152
  57.7 2.3 %constant_dynamic-update-slice_fusion.3 = bf16[5120,512]{1,0:T(8,128)(2,1)} fusion(bf16[5120,512]{1,0:T(8,128)(2,1)} %constant_dynamic-update-slice_fusion.4, bf16[1024,512]{1,0:T(8,128)(2,1)} %collective-permute-done), kind=kLoop, calls=%fused_computation.40 | loop fusion | bytes 2097152
  63.2 5.3 %gather_fusion = bf16[28,128,512]{2,1,0:T(8,128)(2,1)} fusion(bf16[40,128,512]{2,1,0:T(8,128)(2,1)} %bitcast.6, s32[1024]{0:T(1024)S(1)} %pad_clamp_fusion), kind=kCustom, calls=%fused_computation | custom fusion | bytes 7340144 | tf_op jit(solution)/shard_map/jit(_take)/gather | solution.py:62
  68.5 3.2 %fusion.2 = f32[28,128,512]{2,1,0:T(8,128)S(1)} fusion(bf16[28,128,512]{2,1,0:T(8,128)(2,1)} %gather_fusion, pred[28]{0:T(512)(128)(4,1)S(1)} %get-tuple-element.7, bf16[1,28,128,128]{3,2,1,0:T(8,128)(2,1)S(1)} %copy-done.4, bf16[28]{0:T(256)(128)(2,1)S(1)} %get-tuple-element.8), kind=kOutput, calls=%fused_computation.3 | convolution fusion | flops 472055808 | bytes 11927636 | tf_op jit(solution)/shard_map/tij,tjd->tid/dot_general | solution.py:65
  71.7 6.9 %fusion.19 = bf16[8,128,512]{2,0,1:T(8,128)(2,1)S(1)} fusion(f32[28,128,512]{2,1,0:T(8,128)S(1)} %fusion.2, s32[28]{0:T(128)S(1)} %subtract_bitcast_fusion), kind=kOutput, calls=%fused_computation.25 | convolution fusion | flops 176685280 | bytes 8388720 | tf_op jit(solution)/shard_map/bt,tid->bid/dot_general | solution.py:68
  81.8 8.2 %reduce.2 = bf16[1024,512]{1,0:T(8,128)(2,1)} reduce(bf16[1024,1,512]{2,1,0:T(2,128)(2,1)S(1)} %bitcast.61, bf16[]{:T(256)} %broadcast.84), dimensions={1}, to_apply=%bitcast.58.reduce_sub_computation | reduce | bytes 2097154
  89.9 2.6 %reshape.111 = bf16[2,2,131072]{2,1,0:T(2,128)(2,1)} reshape(bf16[1024,512]{1,0:T(8,128)(2,1)} %reduce.2) | data formatting | bytes 2097152
  92.6 4.6 %all-to-all-start = ((bf16[2,2,131072]{2,1,0:T(2,128)(2,1)}), bf16[2,2,131072]{2,1,0:T(2,128)(2,1)}, u32[]{:S(2)}, u32[]{:S(2)}) async-start(bf16[2,2,131072]{2,1,0:T(2,128)(2,1)} %reshape.111), calls=%async_computation | async-start | bytes 2097152 | tf_op jit(solution)/shard_map/all_to_all | solution.py:72
  97.2 9.2 %all-to-all-done = bf16[2,2,131072]{2,1,0:T(2,128)(2,1)} async-done(((bf16[2,2,131072]{2,1,0:T(2,128)(2,1)}), bf16[2,2,131072]{2,1,0:T(2,128)(2,1)}, u32[]{:S(2)}, u32[]{:S(2)}) %all-to-all-start) | async-done | bytes 1048608 | tf_op jit(solution)/shard_map/all_to_all | solution.py:72
  106.5 2.0 %reshape.112 = bf16[1024,1,512]{2,1,0:T(2,128)(2,1)S(1)} reshape(bf16[2,2,131072]{2,1,0:T(2,128)(2,1)} %all-to-all-done) | data formatting | bytes 2097152
  110.5 2.1 %reshape.108 = bf16[2,512,8,64]{3,2,1,0:T(8,128)(2,1)} reshape(bf16[1024,512]{1,0:T(8,128)(2,1)S(1)} %convolution_convert_fusion.3) | data formatting | bytes 2097152 | tf_op jit(solution)/shard_map/reshape | solution.py:78
  113.4 2.1 %reshape.109 = bf16[2,512,8,64]{3,2,1,0:T(8,128)(2,1)} reshape(bf16[1024,512]{1,0:T(8,128)(2,1)S(1)} %convolution_convert_fusion.2) | data formatting | bytes 2097152 | tf_op jit(solution)/shard_map/reshape | solution.py:76
  116.3 2.1 %reshape.110 = bf16[2,512,8,64]{3,2,1,0:T(8,128)(2,1)} reshape(bf16[1024,512]{1,0:T(8,128)(2,1)S(1)} %convolution_convert_fusion.1) | data formatting | bytes 2097152 | tf_op jit(solution)/shard_map/reshape | solution.py:77
  118.4 8.6 %fusion.14 = f32[512,8,2,2]{2,3,1,0:T(2,128)} fusion(bf16[2,512,8,64]{3,2,1,0:T(8,128)(2,1)} %reshape.110, bf16[2,512,8,64]{3,2,1,0:T(8,128)(2,1)} %reshape.109), kind=kOutput, calls=%fused_computation.20 | convolution fusion | flops 2097152 | bytes 2162688 | tf_op jit(solution)/shard_map/snhd,unhd->nhsu/dot_general | solution.py:79
  127.0 3.7 %copy.46 = f32[512,8,2,2]{0,1,3,2:T(8,128)S(1)} copy(f32[512,8,2,2]{2,3,1,0:T(2,128)} %fusion.14) | data formatting | bytes 131072 | tf_op jit(solution)/shard_map/snhd,unhd->nhsu/dot_general | solution.py:79
  131.0 2.9 %copy.48 = bf16[512,8,2,2]{3,2,1,0:T(2,128)(2,1)} copy(bf16[512,8,2,2]{0,1,3,2:T(8,128)(2,1)S(1)} %divide_convert_fusion) | data formatting | bytes 65536 | tf_op jit(solution)/shard_map/convert_element_type | solution.py:84
  133.9 8.0 %fusion.5 = bf16[2,512,8,64]{3,0,2,1:T(2,128)(2,1)} fusion(bf16[512,8,2,2]{3,2,1,0:T(2,128)(2,1)} %copy.48, bf16[2,512,8,64]{3,2,1,0:T(8,128)(2,1)} %reshape.108), kind=kOutput, calls=%fused_computation.10 | convolution fusion | flops 2621440 | bytes 2129920 | tf_op jit(solution)/shard_map/nhsu,unhd->snhd/dot_general | solution.py:85
  141.9 5.1 %copy.49 = bf16[2,512,8,64]{1,0,3,2:T(2,128)(2,1)S(1)} copy(bf16[2,512,8,64]{3,0,2,1:T(2,128)(2,1)} %fusion.5) | data formatting | bytes 2097152 | tf_op jit(solution)/shard_map/convert_element_type | solution.py:86
  (46 shorter events, 16.1 us)
Async XLA Ops:
  0.0 78.9 %copy-start = (bf16[512,512]{1,0:T(8,128)(2,1)S(1)}, bf16[512,512]{1,0:T(8,128)(2,1)}, u32[]{:S(2)}) copy-start(bf16[512,512]{1,0:T(8,128)(2,1)} %param.16) | copy-start | bytes 1572868
  0.0 27.8 %collective-permute-start = (bf16[1024,512]{1,0:T(8,128)(2,1)}, bf16[1024,512]{1,0:T(8,128)(2,1)}, u32[]{:S(2)}, u32[]{:S(2)}) collective-permute-start(bf16[1024,512]{1,0:T(8,128)(2,1)} %bitcast.63), channel_id=1, source_target_pairs={{0,1},{1,2},{2,3},{3,4},{4,5},{5,6},{6,7},{7,8},{8,9},{9,10},{10,1... | collective-permute-start | bytes 3145736 | tf_op jit(solution)/shard_map/ppermute | solution.py:13
  2.1 35.9 %collective-permute-start.2 = (bf16[1024,512]{1,0:T(8,128)(2,1)}, bf16[1024,512]{1,0:T(8,128)(2,1)S(1)}, u32[]{:S(2)}, u32[]{:S(2)}) collective-permute-start(bf16[1024,512]{1,0:T(8,128)(2,1)} %bitcast.64), channel_id=1, source_target_pairs={{1,0},{2,1},{3,2},{4,3},{5,4},{6,5},{7,6},{8,7},{9,8},{10,9},{11,1... | collective-permute-start | bytes 3145736 | tf_op jit(solution)/shard_map/ppermute | solution.py:13
  27.8 27.7 %collective-permute-start.1 = (bf16[1024,512]{1,0:T(8,128)(2,1)}, bf16[1024,512]{1,0:T(8,128)(2,1)}, u32[]{:S(2)}, u32[]{:S(2)}) collective-permute-start(bf16[1024,512]{1,0:T(8,128)(2,1)} %collective-permute-done), channel_id=1, source_target_pairs={{0,1},{1,2},{2,3},{3,4},{4,5},{5,6},{6,7},{7,8},{8,9},{9,10},{10,1... | collective-permute-start | bytes 3145736 | tf_op jit(solution)/shard_map/ppermute | solution.py:13
  38.0 24.2 %collective-permute-start.3 = (bf16[1024,512]{1,0:T(8,128)(2,1)S(1)}, bf16[1024,512]{1,0:T(8,128)(2,1)S(1)}, u32[]{:S(2)}, u32[]{:S(2)}) collective-permute-start(bf16[1024,512]{1,0:T(8,128)(2,1)S(1)} %collective-permute-done.2), channel_id=1, source_target_pairs={{1,0},{2,1},{3,2},{4,3},{5,4},{6,5},{7,6},{8,7},{9,8},{10,9},{11,1... | collective-permute-start | bytes 3145736 | tf_op jit(solution)/shard_map/ppermute | solution.py:13
  43.7 16.4 %copy-start.3 = (bf16[1,1024,512]{2,1,0:T(8,128)(2,1)S(1)}, bf16[1,1024,512]{2,1,0:T(8,128)(2,1)}, u32[]{:S(2)}) copy-start(bf16[1,1024,512]{2,1,0:T(8,128)(2,1)} %param.11) | copy-start | bytes 3145732
  63.2 5.3 %copy-start.4 = (bf16[1,28,128,128]{3,2,1,0:T(8,128)(2,1)S(1)}, bf16[1,28,128,128]{3,2,1,0:T(8,128)(2,1)}, u32[]{:S(2)}) copy-start(bf16[1,28,128,128]{3,2,1,0:T(8,128)(2,1)} %param.14) | copy-start | bytes 2752516
  92.6 13.9 %all-to-all-start = ((bf16[2,2,131072]{2,1,0:T(2,128)(2,1)}), bf16[2,2,131072]{2,1,0:T(2,128)(2,1)}, u32[]{:S(2)}, u32[]{:S(2)}) async-start(bf16[2,2,131072]{2,1,0:T(2,128)(2,1)} %reshape.111), calls=%async_computation | async-start | bytes 2097152 | tf_op jit(solution)/shard_map/all_to_all | solution.py:72
  108.4 1.2 copy-start.5
  108.4 1.2 copy-start.9
  108.7 1.0 copy-start.1
  110.5 2.1 %copy-start.2 = (bf16[1,1024,512]{2,1,0:T(8,128)(2,1)S(1)}, bf16[1,1024,512]{2,1,0:T(8,128)(2,1)}, u32[]{:S(2)}) copy-start(bf16[1,1024,512]{2,1,0:T(8,128)(2,1)} %copy-done.1) | copy-start | bytes 3145732
  110.5 2.1 %copy-start.6 = (bf16[512,512]{1,0:T(8,128)(2,1)S(1)}, bf16[512,512]{1,0:T(8,128)(2,1)}, u32[]{:S(2)}) copy-start(bf16[512,512]{1,0:T(8,128)(2,1)} %param.18) | copy-start | bytes 1572868
  113.4 2.1 %copy-start.7 = (bf16[512,512]{1,0:T(8,128)(2,1)S(1)}, bf16[512,512]{1,0:T(8,128)(2,1)}, u32[]{:S(2)}) copy-start(bf16[512,512]{1,0:T(8,128)(2,1)} %param.19) | copy-start | bytes 1572868
  141.9 5.3 %copy-start.8 = (bf16[512,512]{1,0:T(8,128)(2,1)S(1)}, bf16[512,512]{1,0:T(8,128)(2,1)}, u32[]{:S(2)}) copy-start(bf16[512,512]{1,0:T(8,128)(2,1)} %param.21) | copy-start | bytes 1572868
where the time goes:
time: 150 us; the launch traced here: 149 us
  waiting for transfers between devices  50.7 us (34%)
  local copies, waits for them, and re-layouts  38.7 us (26%)
  matrix products  31.6 us (21%)
  starting transfers between devices  15.9 us (11%)
  other arithmetic  11.2 us (7%)
    ppermute x4, waiting for transfers between devices, from_behind(): return lax.ppermute(block, axis, route)  41.5 us
    unnamed x28, local copies, waits for them, and re-layouts  12.5 us
    ppermute x4, starting transfers between devices, from_behind(): return lax.ppermute(block, axis, route)  11.3 us
    all_to_all x1, waiting for transfers between devices, local(): lax.all_to_all(hidden[None], 'snap', split_axis=1, concat_axis=0, tiled=T...  9.24 us
    dot_general x1, matrix products, local(): jnp.einsum('snhd,unhd->nhsu', query, key, preferred_element_type=jnp.floa...  8.64 us
    unnamed x1, other arithmetic  8.15 us
    dot_general x1, matrix products, local(): jnp.einsum('nhsu,unhd->snhd', weights, value, preferred_element_type=jnp....  8.01 us
    dot_general x1, matrix products, local(): jnp.einsum('bt,tid->bid', select, prod, precision=lax.Precision.HIGHEST)  6.9 us
  transfers between devices with their start and end apart: 5, of which 4 were waited for; matrix products, arithmetic and copies ran while one was open for 6% of the time, Pallas kernels for 0%

commit v1 on v0

v1 whole, which is shorter than its diff:
```python
import functools

import jax
import jax.numpy as jnp
from jax import lax
from jax.experimental import pallas as pl
from jax.experimental.pallas import tpu as pltpu
from jax.sharding import PartitionSpec as P

HEAD_DIM = 64
GROUPS = ((0,), (1,), (2,), (3,))
CHUNK = 128

VMEM_SPEC = pl.BlockSpec(memory_space=pltpu.VMEM)
SMEM_SPEC = pl.BlockSpec(memory_space=pltpu.SMEM)


def routes(nodes):
    far = nodes // 4
    across = [(n, n ^ 2) for n in range(nodes)]
    beside = [(n, n ^ 1) for n in range(nodes)]
    onward = []
    for n in range(nodes):
        group, within = divmod(n, 4)
        step = 1 if within < 2 else -1
        onward.append((n, ((group + step) % far) * 4 + within))
    return across, beside, onward


def graph_kernel(blocks_dev, snaps, sources, rows_ref, cols_ref, count_ref, me_ref, tiles_ref, *refs):
    source_refs, refs = refs[:sources], refs[sources:]
    out_refs, (window, total) = refs[:snaps], refs[snaps:]
    slots, tile, _ = tiles_ref.shape
    here = rows_ref[0, 0] // blocks_dev
    lead = (here // 2) % 2
    core = here % 2
    low = 3 - lead
    high = 2 + lead
    order = [
        low,
        jnp.where(core == 0, 4, 1),
        0,
        jnp.where(core == 0, 1, 4),
        high,
    ]
    span = source_refs[0].shape[0] // tile
    for number, ref in enumerate(source_refs):
        for block in range(span):
            window[number * span + block] = ref[block * tile : (block + 1) * tile, :]
    total[...] = jnp.zeros_like(total)
    first = (here - 2) * blocks_dev
    live = count_ref[0, 0]
    for slot in range(slots):
        col = cols_ref[0, slot] - first
        side = col // blocks_dev
        number = order[4]
        for index in range(4):
            number = jnp.where(side == index, order[index], number)
        block = number * span + col % blocks_dev
        row = jnp.where(slot < live, rows_ref[0, slot] - here * blocks_dev, blocks_dev)
        total[row] += jnp.dot(tiles_ref[slot], window[block], preferred_element_type=jnp.float32)
    each = blocks_dev // snaps
    me = me_ref[0]
    for distance, out_ref in enumerate(out_refs):
        part = lax.rem(me + distance, snaps)
        for block in range(each):
            out_ref[block * tile : (block + 1) * tile, :] = total[part * each + block].astype(out_ref.dtype)


def graph_call(rows, cols, count, me, tiles, sources, snaps, blocks_dev):
    width = sources[0].shape[1]
    slots, tile, _ = tiles.shape
    nodes_dev = sources[0].shape[0]
    part = nodes_dev // snaps
    return pl.pallas_call(
        functools.partial(graph_kernel, blocks_dev, snaps, len(sources)),
        out_shape=[jax.ShapeDtypeStruct((part, width), jnp.bfloat16)] * snaps,
        in_specs=[SMEM_SPEC] * 4 + [VMEM_SPEC] * (1 + len(sources)),
        out_specs=[VMEM_SPEC] * snaps,
        scratch_shapes=[
            pltpu.VMEM((len(sources) * blocks_dev, tile, width), jnp.bfloat16),
            pltpu.VMEM((blocks_dev + 1, tile, width), jnp.float32),
        ],
        compiler_params=pltpu.CompilerParams(vmem_limit_bytes=16 << 20),
        cost_estimate=pl.CostEstimate(
            flops=2 * slots * tile * tile * width, bytes_accessed=4 << 20, transcendentals=0
        ),
        name="graph",
    )(rows, cols, count, me, tiles, *sources)


def layer_kernel(snaps, groups, me_ref, gain_ref, wg_ref, wq_ref, wk_ref, wv_ref, wo_ref, *refs):
    feat_refs, refs = refs[:snaps], refs[snaps:]
    agg_refs, refs = refs[: snaps * groups], refs[snaps * groups :]
    out_ref, hidden, normed, query, key, value, context, heads = refs
    _, part, width = out_ref.shape
    me = me_ref[0]
    gain = gain_ref[...]
    step = min(part, 128)
    for distance in range(snaps):
        snap = lax.rem(me - distance + snaps, snaps)
        feat_ref = feat_refs[distance]
        mine = agg_refs[distance * groups : (distance + 1) * groups]

        @pl.loop(0, part // step)
        def _(index):
            at = pl.ds(pl.multiple_of(index * step, step), step)
            agg = jnp.concatenate([ref[at, :] for ref in mine], axis=1)
            mixed = jnp.dot(agg, wg_ref[...], preferred_element_type=jnp.float32)
            hid = (feat_ref[at, :].astype(jnp.float32) + jnp.maximum(mixed, 0.0)).astype(jnp.bfloat16)
            hidden[snap, at, :] = hid
            val = hid.astype(jnp.float32)
            mean = jnp.mean(val, axis=-1, keepdims=True)
            centred = val - mean
            variance = jnp.mean(centred * centred, axis=-1, keepdims=True)
            normed[snap, at, :] = (centred * lax.rsqrt(variance + 1e-05) * gain).astype(jnp.bfloat16)

    head_row = lax.broadcasted_iota(jnp.int32, (width, width), 0) // HEAD_DIM
    head_col = lax.broadcasted_iota(jnp.int32, (width, width), 1) // HEAD_DIM
    heads[...] = jnp.where(head_row == head_col, 1.0, 0.0).astype(jnp.bfloat16)

    for snap in range(snaps):
        big = min(part, 256)

        @pl.loop(0, part // big)
        def _(index):
            at = pl.ds(pl.multiple_of(index * big, big), big)
            rows = normed[snap, at, :]
            query[snap, at, :] = jnp.dot(rows, wq_ref[...], preferred_element_type=jnp.float32).astype(jnp.bfloat16)
            key[snap, at, :] = jnp.dot(rows, wk_ref[...], preferred_element_type=jnp.float32).astype(jnp.bfloat16)
            value[snap, at, :] = jnp.dot(rows, wv_ref[...], preferred_element_type=jnp.float32).astype(jnp.bfloat16)

    @pl.loop(0, part // step)
    def _(index):
        at = pl.ds(pl.multiple_of(index * step, step), step)
        for snap in range(snaps):
            que = query[snap, at, :].astype(jnp.float32)
            scores = []
            for other in range(snap + 1):
                exact = que * key[other, at, :].astype(jnp.float32)
                high = exact.astype(jnp.bfloat16)
                low = (exact - high.astype(jnp.float32)).astype(jnp.bfloat16)
                score = jnp.dot(high, heads[...], preferred_element_type=jnp.float32)
                score += jnp.dot(low, heads[...], preferred_element_type=jnp.float32)
                scores.append(score * HEAD_DIM**-0.5)
            peak = functools.reduce(jnp.maximum, scores)
            powers = [jnp.exp(score - peak) for score in scores]
            whole = functools.reduce(jnp.add, powers)
            mixed = jnp.zeros_like(whole)
            for other in range(snap + 1):
                weight = (powers[other] / whole).astype(jnp.bfloat16).astype(jnp.float32)
                mixed += weight * value[other, at, :].astype(jnp.float32)
            context[snap, at, :] = mixed.astype(jnp.bfloat16)

    for snap in range(snaps):
        big = min(part, 256)

        @pl.loop(0, part // big)
        def _(index):
            at = pl.ds(pl.multiple_of(index * big, big), big)
            made = jnp.dot(context[snap, at, :], wo_ref[...], preferred_element_type=jnp.float32)
            out_ref[snap, at, :] = (hidden[snap, at, :].astype(jnp.float32) + made).astype(jnp.bfloat16)


def layer_call(me, gain, weights, feats, aggs, snaps):
    part, width = feats[0].shape
    groups = len(aggs) // snaps
    full = (snaps, part, width)
    return pl.pallas_call(
        functools.partial(layer_kernel, snaps, groups),
        out_shape=jax.ShapeDtypeStruct(full, jnp.bfloat16),
        in_specs=[SMEM_SPEC] + [VMEM_SPEC] * (1 + len(weights) + len(feats) + len(aggs)),
        out_specs=VMEM_SPEC,
        scratch_shapes=[pltpu.VMEM(full, jnp.bfloat16)] * 6 + [pltpu.VMEM((width, width), jnp.bfloat16)],
        compiler_params=pltpu.CompilerParams(vmem_limit_bytes=32 << 20),
        cost_estimate=pl.CostEstimate(
            flops=10 * snaps * part * width * width, bytes_accessed=8 << 20, transcendentals=0
        ),
        name="layer",
    )(me, gain, *weights, *feats, *aggs)


def local(
    features,
    tile_rows,
    tile_cols,
    tile_values,
    tile_count,
    w_graph,
    norm_gain,
    w_query,
    w_key,
    w_value,
    w_out,
):
    feats = features[0]
    nodes_dev, width = feats.shape
    tile = tile_values.shape[-1]
    blocks_dev = nodes_dev // tile
    snaps = lax.axis_size("snap")
    part = nodes_dev // snaps
    across, beside, onward = routes(lax.axis_size("node"))
    here = lax.axis_index("node")
    me = lax.axis_index("snap").astype(jnp.int32)
    me_ref = me.reshape(1)
    shifts = [[(i, (i + d) % snaps) for i in range(snaps)] for d in range(snaps)]

    chunks = width // CHUNK
    mine = [feats[:, c * CHUNK : (c + 1) * CHUNK] for c in range(chunks)]
    near = [lax.ppermute(block, "node", across) for block in mine]
    partner = lax.ppermute(feats, "node", beside)
    parts = feats.reshape(snaps, part, width)
    own_feats = [lax.dynamic_index_in_dim(parts, lax.rem(me + d, snaps), 0, keepdims=False) for d in range(snaps)]
    feat_parts = [own_feats[0]] + [lax.ppermute(own_feats[d], "snap", shifts[d]) for d in range(1, snaps)]
    far = [lax.ppermute(block, "node", onward) for block in near]
    same = (here // 2) % 2 == here % 2
    received = [[] for _ in range(snaps)]
    for group in GROUPS:
        join = lambda blocks: jnp.concatenate([blocks[c] for c in group], axis=1)
        close, away = join(near), join(far)
        relayed = lax.ppermute(jnp.where(same, close, away), "node", beside)
        columns = slice(group[0] * CHUNK, (group[-1] + 1) * CHUNK)
        sources = [feats[:, columns], partner[:, columns], close, away, relayed]
        outs = graph_call(tile_rows, tile_cols, tile_count, me_ref, tile_values[0], sources, snaps, blocks_dev)
        received[0].append(outs[0])
        for d in range(1, snaps):
            received[d].append(lax.ppermute(outs[d], "snap", shifts[d]))
    aggs = [agg for rows in received for agg in rows]
    return layer_call(
        me_ref,
        norm_gain.reshape(1, width),
        (w_graph, w_query, w_key, w_value, w_out),
        feat_parts,
        aggs,
        snaps,
    )


def solution(mesh):
    in_specs = (
        P("snap", "node", None),
        P("snap", "node"),
        P("snap", "node"),
        P("snap", "node", None, None),
        P("snap", "node"),
        P(),
        P(),
        P(),
        P(),
        P(),
        P(),
    )
    out_specs = P(None, ("node", "snap"), None)
    return jax.shard_map(local, mesh=mesh, in_specs=in_specs, out_specs=out_specs, check_vma=False)
```

time: 150 us -> 72.1 us (0.48)
  the two profiles are of different devices: /device:TPU:12 before, /device:TPU:0 now
where the time goes in v1:
time: 72.1 us; the launch traced here: 71.9 us
  waiting for transfers between devices  29.6 us (41%)
  starting transfers between devices  19.6 us (27%)
  Pallas kernels  15.7 us (22%)
  local copies, waits for them, and re-layouts  5.95 us (8%)
  between operations  0.84 us (1%)
    ppermute x4, waiting for transfers between devices, local(): near = [lax.ppermute(block, 'node', across) for block in mine]  12.2 us
    ppermute x4, waiting for transfers between devices, local(): far = [lax.ppermute(block, 'node', onward) for block in near]  11.3 us
    pallas_call x1, Pallas kernels, layer_call(): pl.pallas_call(functools.partial(layer_kernel, snaps, groups), out_shape=...  11 us
    ppermute x4, starting transfers between devices, local(): far = [lax.ppermute(block, 'node', onward) for block in near]  7.53 us
    ppermute x4, waiting for transfers between devices, local(): received[d].append(lax.ppermute(outs[d], 'snap', shifts[d]))  6.1 us
    ppermute x4, starting transfers between devices, local(): near = [lax.ppermute(block, 'node', across) for block in mine]  5.16 us
    pallas_call x4, Pallas kernels, graph_call(): pl.pallas_call(functools.partial(graph_kernel, blocks_dev, snaps, len(sou...  4.69 us
    ppermute x4, starting transfers between devices, local(): received[d].append(lax.ppermute(outs[d], 'snap', shifts[d]))  4.31 us
  transfers between devices with their start and end apart: 18, of which 9 were waited for; matrix products, arithmetic and copies ran while one was open for 5% of the time, Pallas kernels for 7%

profile of v1, /device:TPU:0, one launch (start us, length us, event | category | flops | bytes accessed | tf_op | source)
XLA Modules:
  0.0 71.9 jit_solution(10850027973575069330)
XLA Ops:
  0.0 1.3 %fusion.1 = (bf16[1024,128]{1,0:T(8,128)(2,1)S(1)}, bf16[1024,128]{1,0:T(8,128)(2,1)S(1)}, bf16[1024,128]{1,0:T(8,128)(2,1)S(1)}, bf16[1024,128]{1,0:T(8,128)(2,1)S(1)}) fusion(bf16[1024,512]{1,0:T(8,128)(2,1)} %bitcast.6), kind=kLoop, calls=%fused_computation.7 | loop fusion | bytes 2097152 | tf_op jit(solution)/shard_map/slice | solution.py:223
  1.3 3.1 %collective-permute-start.11 = (bf16[1024,128]{1,0:T(8,128)(2,1)S(1)}, bf16[1024,128]{1,0:T(8,128)(2,1)S(1)}, u32[]{:S(2)}, u32[]{:S(2)}) collective-permute-start(bf16[1024,128]{1,0:T(8,128)(2,1)S(1)} %get-tuple-element.25.refs_0_), channel_id=1, source_target_pairs={{0,2},{1,3},{2,0},{3,1},{4,6},{5,7},{6,4},{7,5},{8,10},{9,11},{10,... | collective-permute-start | bytes 786440 | tf_op jit(solution)/shard_map/ppermute | solution.py:210
  4.4 1.9 %collective-permute-start.5 = (bf16[1024,128]{1,0:T(8,128)(2,1)S(1)}, bf16[1024,128]{1,0:T(8,128)(2,1)S(1)}, u32[]{:S(2)}, u32[]{:S(2)}) collective-permute-start(bf16[1024,128]{1,0:T(8,128)(2,1)S(1)} %get-tuple-element.27.refs_0_), channel_id=1, source_target_pairs={{0,2},{1,3},{2,0},{3,1},{4,6},{5,7},{6,4},{7,5},{8,10},{9,11},{10,... | collective-permute-start | bytes 786440 | tf_op jit(solution)/shard_map/ppermute | solution.py:210
  6.5 5.0 %collective-permute-done.11.refs_2_ = bf16[1024,128]{1,0:T(8,128)(2,1)S(1)} collective-permute-done((bf16[1024,128]{1,0:T(8,128)(2,1)S(1)}, bf16[1024,128]{1,0:T(8,128)(2,1)S(1)}, u32[]{:S(2)}, u32[]{:S(2)}) %collective-permute-start.11) | collective-permute-done | bytes 262176 | tf_op jit(solution)/shard_map/ppermute | solution.py:210
  11.5 2.1 %collective-permute-start.12 = (bf16[1024,128]{1,0:T(8,128)(2,1)S(1)}, bf16[1024,128]{1,0:T(8,128)(2,1)S(1)}, u32[]{:S(2)}, u32[]{:S(2)}) collective-permute-start(bf16[1024,128]{1,0:T(8,128)(2,1)S(1)} %collective-permute-done.11.refs_2_), channel_id=1, source_target_pairs={{0,4},{1,5},{2,14},{3,15},{4,8},{5,9},{6,2},{7,3},{8,12},{9,13},{1... | collective-permute-start | bytes 786440 | tf_op jit(solution)/shard_map/ppermute | solution.py:215
  13.6 3.5 %collective-permute-done.8.refs_2_ = bf16[1024,128]{1,0:T(8,128)(2,1)S(1)} collective-permute-done((bf16[1024,128]{1,0:T(8,128)(2,1)S(1)}, bf16[1024,128]{1,0:T(8,128)(2,1)S(1)}, u32[]{:S(2)}, u32[]{:S(2)}) %collective-permute-start.8) | collective-permute-done | bytes 262176 | tf_op jit(solution)/shard_map/ppermute | solution.py:210
  17.1 2.1 %collective-permute-start.9 = (bf16[1024,128]{1,0:T(8,128)(2,1)S(1)}, bf16[1024,128]{1,0:T(8,128)(2,1)S(1)}, u32[]{:S(2)}, u32[]{:S(2)}) collective-permute-start(bf16[1024,128]{1,0:T(8,128)(2,1)S(1)} %collective-permute-done.8.refs_2_), channel_id=1, source_target_pairs={{0,4},{1,5},{2,14},{3,15},{4,8},{5,9},{6,2},{7,3},{8,12},{9,13},{1... | collective-permute-start | bytes 786440 | tf_op jit(solution)/shard_map/ppermute | solution.py:215
  19.2 2.1 %dynamic-slice_bitcast_fusion = (bf16[512,512]{1,0:T(8,128)(2,1)}, bf16[512,512]{1,0:T(8,128)(2,1)S(1)}) fusion(bf16[2,512,512]{2,1,0:T(8,128)(2,1)} %bitcast.2, s32[]{:T(128)S(6)} %select_n.43, s32[]{:T(128)S(6)} %select_n.42), kind=kLoop, calls=%fused_computation | loop fusion | bytes 2097160 | tf_op jit(solution)/shard_map/jit(dynamic_index_in_dim)/squeeze | solution.py:213
  22.7 2.0 %collective-permute-start = (bf16[512,512]{1,0:T(8,128)(2,1)}, bf16[512,512]{1,0:T(8,128)(2,1)S(1)}, u32[]{:S(2)}, u32[]{:S(2)}) collective-permute-start(bf16[512,512]{1,0:T(8,128)(2,1)} %get-tuple-element.29), channel_id=1, source_target_pairs={{0,16},{16,0},{1,17},{17,1},{2,18},{18,2},{3,19},{19,3},{4,20},{20... | collective-permute-start | bytes 1572872 | tf_op jit(solution)/shard_map/ppermute | solution.py:214
  24.7 2.8 %collective-permute-done.2.refs_2_ = bf16[1024,128]{1,0:T(8,128)(2,1)S(1)} collective-permute-done((bf16[1024,128]{1,0:T(8,128)(2,1)S(1)}, bf16[1024,128]{1,0:T(8,128)(2,1)S(1)}, u32[]{:S(2)}, u32[]{:S(2)}) %collective-permute-start.2) | collective-permute-done | bytes 262176 | tf_op jit(solution)/shard_map/ppermute | solution.py:210
  27.5 1.8 %collective-permute-start.6 = (bf16[1024,128]{1,0:T(8,128)(2,1)S(1)}, bf16[1024,128]{1,0:T(8,128)(2,1)S(1)}, u32[]{:S(2)}, u32[]{:S(2)}) collective-permute-start(bf16[1024,128]{1,0:T(8,128)(2,1)S(1)} %collective-permute-done.5.refs_2_), channel_id=1, source_target_pairs={{0,4},{1,5},{2,14},{3,15},{4,8},{5,9},{6,2},{7,3},{8,12},{9,13},{1... | collective-permute-start | bytes 786440 | tf_op jit(solution)/shard_map/ppermute | solution.py:215
  29.3 1.6 %collective-permute-start.3 = (bf16[1024,128]{1,0:T(8,128)(2,1)S(1)}, bf16[1024,128]{1,0:T(8,128)(2,1)S(1)}, u32[]{:S(2)}, u32[]{:S(2)}) collective-permute-start(bf16[1024,128]{1,0:T(8,128)(2,1)S(1)} %collective-permute-done.2.refs_2_), channel_id=1, source_target_pairs={{0,4},{1,5},{2,14},{3,15},{4,8},{5,9},{6,2},{7,3},{8,12},{9,13},{1... | collective-permute-start | bytes 786440 | tf_op jit(solution)/shard_map/ppermute | solution.py:215
  31.0 7.4 %collective-permute-done.6.refs_3_ = bf16[1024,128]{1,0:T(8,128)(2,1)S(1)} collective-permute-done((bf16[1024,128]{1,0:T(8,128)(2,1)S(1)}, bf16[1024,128]{1,0:T(8,128)(2,1)S(1)}, u32[]{:S(2)}, u32[]{:S(2)}) %collective-permute-start.6) | collective-permute-done | bytes 262176 | tf_op jit(solution)/shard_map/ppermute | solution.py:215
  38.5 3.9 %collective-permute-done.3.refs_3_ = bf16[1024,128]{1,0:T(8,128)(2,1)S(1)} collective-permute-done((bf16[1024,128]{1,0:T(8,128)(2,1)S(1)}, bf16[1024,128]{1,0:T(8,128)(2,1)S(1)}, u32[]{:S(2)}, u32[]{:S(2)}) %collective-permute-start.3) | collective-permute-done | bytes 262176 | tf_op jit(solution)/shard_map/ppermute | solution.py:215
  43.0 1.3 %fusion = (bf16[1024,128]{1,0:T(8,128)(2,1)S(1)}, bf16[1024,128]{1,0:T(8,128)(2,1)S(1)}, bf16[1024,128]{1,0:T(8,128)(2,1)S(1)}, bf16[1024,128]{1,0:T(8,128)(2,1)S(1)}) fusion(bf16[1024,512]{1,0:T(8,128)(2,1)} %collective-permute-done.1), kind=kLoop, calls=%fused_computation.6 | loop fusion | bytes 2097152 | tf_op jit(solution)/shard_map/slice | solution.py:223
  45.0 1.2 %graph.7 = (bf16[512,128]{1,0:T(8,128)(2,1)S(1)}, bf16[512,128]{1,0:T(8,128)(2,1)S(1)}) custom-call(s32[1,28]{1,0:T(1,128)S(1)} %copy-done.1, s32[1,28]{1,0:T(1,128)S(1)} %copy-done.2, s32[1,1]{1,0:T(1,128)S(6)} %copy.12.count_ref, s32[1]{0:T(128)} %bitcast.me_ref, bf16[28,128,128]{2,1,0:T(8,128)(2,1)S(1)} %bitcast.9, ...), custom_call_target="tpu_custom_call" | custom-call | flops 117440512 | bytes 4194304 | tf_op jit(solution)/shard_map/graph/pallas_call | solution.py:75
  46.2 1.6 %collective-permute-start.17 = (bf16[512,128]{1,0:T(8,128)(2,1)S(1)}, bf16[512,128]{1,0:T(8,128)(2,1)S(1)}, u32[]{:S(2)}, u32[]{:S(2)}) collective-permute-start(bf16[512,128]{1,0:T(8,128)(2,1)S(1)} %get-tuple-element.20), channel_id=1, source_target_pairs={{0,16},{16,0},{1,17},{17,1},{2,18},{18,2},{3,19},{19,3},{4,20},{20... | collective-permute-start | bytes 393224 | tf_op jit(solution)/shard_map/ppermute | solution.py:227
  49.5 1.2 %graph.5 = (bf16[512,128]{1,0:T(8,128)(2,1)S(1)}, bf16[512,128]{1,0:T(8,128)(2,1)S(1)}) custom-call(s32[1,28]{1,0:T(1,128)S(1)} %copy-done.1, s32[1,28]{1,0:T(1,128)S(1)} %copy-done.2, s32[1,1]{1,0:T(1,128)S(6)} %copy.12.count_ref, s32[1]{0:T(128)} %bitcast.me_ref, bf16[28,128,128]{2,1,0:T(8,128)(2,1)S(1)} %bitcast.11, ...), custom_call_target="tpu_custom_call" | custom-call | flops 117440512 | bytes 4194304 | tf_op jit(solution)/shard_map/graph/pallas_call | solution.py:75
  50.7 1.6 %collective-permute-start.15 = (bf16[512,128]{1,0:T(8,128)(2,1)S(1)}, bf16[512,128]{1,0:T(8,128)(2,1)S(1)}, u32[]{:S(2)}, u32[]{:S(2)}) collective-permute-start(bf16[512,128]{1,0:T(8,128)(2,1)S(1)} %get-tuple-element.18), channel_id=1, source_target_pairs={{0,16},{16,0},{1,17},{17,1},{2,18},{18,2},{3,19},{19,3},{4,20},{20... | collective-permute-start | bytes 393224 | tf_op jit(solution)/shard_map/ppermute | solution.py:227
  52.3 1.2 %graph.4 = (bf16[512,128]{1,0:T(8,128)(2,1)S(1)}, bf16[512,128]{1,0:T(8,128)(2,1)S(1)}) custom-call(s32[1,28]{1,0:T(1,128)S(1)} %copy-done.1, s32[1,28]{1,0:T(1,128)S(1)} %copy-done.2, s32[1,1]{1,0:T(1,128)S(6)} %copy.12.count_ref, s32[1]{0:T(128)} %bitcast.me_ref, bf16[28,128,128]{2,1,0:T(8,128)(2,1)S(1)} %bitcast.12, ...), custom_call_target="tpu_custom_call" | custom-call | flops 117440512 | bytes 4194304 | tf_op jit(solution)/shard_map/graph/pallas_call | solution.py:75
  54.1 1.3 %collective-permute-done.16.refs_8_ = bf16[512,128]{1,0:T(8,128)(2,1)S(1)} collective-permute-done((bf16[512,128]{1,0:T(8,128)(2,1)S(1)}, bf16[512,128]{1,0:T(8,128)(2,1)S(1)}, u32[]{:S(2)}, u32[]{:S(2)}) %collective-permute-start.16) | collective-permute-done | bytes 131104 | tf_op jit(solution)/shard_map/ppermute | solution.py:227
  55.3 2.8 %collective-permute-done.15.refs_7_ = bf16[512,128]{1,0:T(8,128)(2,1)S(1)} collective-permute-done((bf16[512,128]{1,0:T(8,128)(2,1)S(1)}, bf16[512,128]{1,0:T(8,128)(2,1)S(1)}, u32[]{:S(2)}, u32[]{:S(2)}) %collective-permute-start.15) | collective-permute-done | bytes 131104 | tf_op jit(solution)/shard_map/ppermute | solution.py:227
  58.2 2.0 %collective-permute-done.14.refs_6_ = bf16[512,128]{1,0:T(8,128)(2,1)S(1)} collective-permute-done((bf16[512,128]{1,0:T(8,128)(2,1)S(1)}, bf16[512,128]{1,0:T(8,128)(2,1)S(1)}, u32[]{:S(2)}, u32[]{:S(2)}) %collective-permute-start.14) | collective-permute-done | bytes 131104 | tf_op jit(solution)/shard_map/ppermute | solution.py:227
  60.8 11.0 %layer.1 = bf16[2,512,512]{2,1,0:T(8,128)(2,1)} custom-call(s32[1]{0:T(128)} %bitcast.me_ref, f32[1,512]{1,0:T(1,128)S(1)} %bitcast.13, bf16[512,512]{1,0:T(8,128)(2,1)S(1)} %copy-done.3, bf16[512,512]{1,0:T(8,128)(2,1)S(1)} %copy-done.4, bf16[512,512]{1,0:T(8,128)(2,1)S(1)} %copy-done.5, bf16[512,512]{1,0:T(8,128)(2,1)S(1)} %copy-done.6, ...), custom_call_target="tpu_custom_call" | custom-call | flops 2684354560 | bytes 8388608 | tf_op jit(solution)/shard_map/layer/pallas_call | solution.py:169
  (42 shorter events, 5.5 us)
Async XLA Ops:
  1.3 10.2 %collective-permute-start.11 = (bf16[1024,128]{1,0:T(8,128)(2,1)S(1)}, bf16[1024,128]{1,0:T(8,128)(2,1)S(1)}, u32[]{:S(2)}, u32[]{:S(2)}) collective-permute-start(bf16[1024,128]{1,0:T(8,128)(2,1)S(1)} %get-tuple-element.25.refs_0_), channel_id=1, source_target_pairs={{0,2},{1,3},{2,0},{3,1},{4,6},{5,7},{6,4},{7,5},{8,10},{9,11},{10,... | collective-permute-start | bytes 786440 | tf_op jit(solution)/shard_map/ppermute | solution.py:210
  4.3 12.8 %collective-permute-start.8 = (bf16[1024,128]{1,0:T(8,128)(2,1)S(1)}, bf16[1024,128]{1,0:T(8,128)(2,1)S(1)}, u32[]{:S(2)}, u32[]{:S(2)}) collective-permute-start(bf16[1024,128]{1,0:T(8,128)(2,1)S(1)} %get-tuple-element.26.refs_0_), channel_id=1, source_target_pairs={{0,2},{1,3},{2,0},{3,1},{4,6},{5,7},{6,4},{7,5},{8,10},{9,11},{10,... | collective-permute-start | bytes 786440 | tf_op jit(solution)/shard_map/ppermute | solution.py:210
  4.4 18.3 %collective-permute-start.5 = (bf16[1024,128]{1,0:T(8,128)(2,1)S(1)}, bf16[1024,128]{1,0:T(8,128)(2,1)S(1)}, u32[]{:S(2)}, u32[]{:S(2)}) collective-permute-start(bf16[1024,128]{1,0:T(8,128)(2,1)S(1)} %get-tuple-element.27.refs_0_), channel_id=1, source_target_pairs={{0,2},{1,3},{2,0},{3,1},{4,6},{5,7},{6,4},{7,5},{8,10},{9,11},{10,... | collective-permute-start | bytes 786440 | tf_op jit(solution)/shard_map/ppermute | solution.py:210
  6.4 21.1 %collective-permute-start.2 = (bf16[1024,128]{1,0:T(8,128)(2,1)S(1)}, bf16[1024,128]{1,0:T(8,128)(2,1)S(1)}, u32[]{:S(2)}, u32[]{:S(2)}) collective-permute-start(bf16[1024,128]{1,0:T(8,128)(2,1)S(1)} %get-tuple-element.28.refs_0_), channel_id=1, source_target_pairs={{0,2},{1,3},{2,0},{3,1},{4,6},{5,7},{6,4},{7,5},{8,10},{9,11},{10,... | collective-permute-start | bytes 786440 | tf_op jit(solution)/shard_map/ppermute | solution.py:210
  11.5 17.8 %collective-permute-start.12 = (bf16[1024,128]{1,0:T(8,128)(2,1)S(1)}, bf16[1024,128]{1,0:T(8,128)(2,1)S(1)}, u32[]{:S(2)}, u32[]{:S(2)}) collective-permute-start(bf16[1024,128]{1,0:T(8,128)(2,1)S(1)} %collective-permute-done.11.refs_2_), channel_id=1, source_target_pairs={{0,4},{1,5},{2,14},{3,15},{4,8},{5,9},{6,2},{7,3},{8,12},{9,13},{1... | collective-permute-start | bytes 786440 | tf_op jit(solution)/shard_map/ppermute | solution.py:215
  13.6 28.9 %collective-permute-start.1 = (bf16[1024,512]{1,0:T(8,128)(2,1)}, bf16[1024,512]{1,0:T(8,128)(2,1)}, u32[]{:S(2)}, u32[]{:S(2)}) collective-permute-start(bf16[1024,512]{1,0:T(8,128)(2,1)} %bitcast.6), channel_id=1, source_target_pairs={{0,1},{1,0},{2,3},{3,2},{4,5},{5,4},{6,7},{7,6},{8,9},{9,8},{10,11... | collective-permute-start | bytes 3145736 | tf_op jit(solution)/shard_map/ppermute | solution.py:211
  17.1 13.8 %collective-permute-start.9 = (bf16[1024,128]{1,0:T(8,128)(2,1)S(1)}, bf16[1024,128]{1,0:T(8,128)(2,1)S(1)}, u32[]{:S(2)}, u32[]{:S(2)}) collective-permute-start(bf16[1024,128]{1,0:T(8,128)(2,1)S(1)} %collective-permute-done.8.refs_2_), channel_id=1, source_target_pairs={{0,4},{1,5},{2,14},{3,15},{4,8},{5,9},{6,2},{7,3},{8,12},{9,13},{1... | collective-permute-start | bytes 786440 | tf_op jit(solution)/shard_map/ppermute | solution.py:215
  22.7 31.3 %collective-permute-start = (bf16[512,512]{1,0:T(8,128)(2,1)}, bf16[512,512]{1,0:T(8,128)(2,1)S(1)}, u32[]{:S(2)}, u32[]{:S(2)}) collective-permute-start(bf16[512,512]{1,0:T(8,128)(2,1)} %get-tuple-element.29), channel_id=1, source_target_pairs={{0,16},{16,0},{1,17},{17,1},{2,18},{18,2},{3,19},{19,3},{4,20},{20... | collective-permute-start | bytes 1572872 | tf_op jit(solution)/shard_map/ppermute | solution.py:214
  27.5 11.0 %collective-permute-start.6 = (bf16[1024,128]{1,0:T(8,128)(2,1)S(1)}, bf16[1024,128]{1,0:T(8,128)(2,1)S(1)}, u32[]{:S(2)}, u32[]{:S(2)}) collective-permute-start(bf16[1024,128]{1,0:T(8,128)(2,1)S(1)} %collective-permute-done.5.refs_2_), channel_id=1, source_target_pairs={{0,4},{1,5},{2,14},{3,15},{4,8},{5,9},{6,2},{7,3},{8,12},{9,13},{1... | collective-permute-start | bytes 786440 | tf_op jit(solution)/shard_map/ppermute | solution.py:215
  29.3 13.1 %collective-permute-start.3 = (bf16[1024,128]{1,0:T(8,128)(2,1)S(1)}, bf16[1024,128]{1,0:T(8,128)(2,1)S(1)}, u32[]{:S(2)}, u32[]{:S(2)}) collective-permute-start(bf16[1024,128]{1,0:T(8,128)(2,1)S(1)} %collective-permute-done.2.refs_2_), channel_id=1, source_target_pairs={{0,4},{1,5},{2,14},{3,15},{4,8},{5,9},{6,2},{7,3},{8,12},{9,13},{1... | collective-permute-start | bytes 786440 | tf_op jit(solution)/shard_map/ppermute | solution.py:215
  30.9 13.4 %collective-permute-start.13 = (bf16[1024,128]{1,0:T(8,128)(2,1)S(1)}, bf16[1024,128]{1,0:T(8,128)(2,1)S(1)}, u32[]{:S(2)}, u32[]{:S(2)}) collective-permute-start(bf16[1024,128]{1,0:T(8,128)(2,1)S(1)} %broadcast_select_fusion), channel_id=1, source_target_pairs={{0,1},{1,0},{2,3},{3,2},{4,5},{5,4},{6,7},{7,6},{8,9},{9,8},{10,11... | collective-permute-start | bytes 786440 | tf_op jit(solution)/shard_map/ppermute | solution.py:221
  38.5 9.3 %collective-permute-start.10 = (bf16[1024,128]{1,0:T(8,128)(2,1)S(1)}, bf16[1024,128]{1,0:T(8,128)(2,1)S(1)}, u32[]{:S(2)}, u32[]{:S(2)}) collective-permute-start(bf16[1024,128]{1,0:T(8,128)(2,1)S(1)} %broadcast_select_fusion.1), channel_id=1, source_target_pairs={{0,1},{1,0},{2,3},{3,2},{4,5},{5,4},{6,7},{7,6},{8,9},{9,8},{10,11... | collective-permute-start | bytes 786440 | tf_op jit(solution)/shard_map/ppermute | solution.py:221
  42.4 7.1 %collective-permute-start.7 = (bf16[1024,128]{1,0:T(8,128)(2,1)S(1)}, bf16[1024,128]{1,0:T(8,128)(2,1)S(1)}, u32[]{:S(2)}, u32[]{:S(2)}) collective-permute-start(bf16[1024,128]{1,0:T(8,128)(2,1)S(1)} %broadcast_select_fusion.2), channel_id=1, source_target_pairs={{0,1},{1,0},{2,3},{3,2},{4,5},{5,4},{6,7},{7,6},{8,9},{9,8},{10,11... | collective-permute-start | bytes 786440 | tf_op jit(solution)/shard_map/ppermute | solution.py:221
  42.4 1.9 %copy-start = (bf16[1,28,128,128]{3,2,1,0:T(8,128)(2,1)S(1)}, bf16[1,28,128,128]{3,2,1,0:T(8,128)(2,1)}, u32[]{:S(2)}) copy-start(bf16[1,28,128,128]{3,2,1,0:T(8,128)(2,1)} %param.14) | copy-start | bytes 2752516
  42.5 9.8 %collective-permute-start.4 = (bf16[1024,128]{1,0:T(8,128)(2,1)S(1)}, bf16[1024,128]{1,0:T(8,128)(2,1)S(1)}, u32[]{:S(2)}, u32[]{:S(2)}) collective-permute-start(bf16[1024,128]{1,0:T(8,128)(2,1)S(1)} %broadcast_select_fusion.3), channel_id=1, source_target_pairs={{0,1},{1,0},{2,3},{3,2},{4,5},{5,4},{6,7},{7,6},{8,9},{9,8},{10,11... | collective-permute-start | bytes 786440 | tf_op jit(solution)/shard_map/ppermute | solution.py:221
  46.2 7.9 %collective-permute-start.17 = (bf16[512,128]{1,0:T(8,128)(2,1)S(1)}, bf16[512,128]{1,0:T(8,128)(2,1)S(1)}, u32[]{:S(2)}, u32[]{:S(2)}) collective-permute-start(bf16[512,128]{1,0:T(8,128)(2,1)S(1)} %get-tuple-element.20), channel_id=1, source_target_pairs={{0,16},{16,0},{1,17},{17,1},{2,18},{18,2},{3,19},{19,3},{4,20},{20... | collective-permute-start | bytes 393224 | tf_op jit(solution)/shard_map/ppermute | solution.py:227
  48.9 6.4 %collective-permute-start.16 = (bf16[512,128]{1,0:T(8,128)(2,1)S(1)}, bf16[512,128]{1,0:T(8,128)(2,1)S(1)}, u32[]{:S(2)}, u32[]{:S(2)}) collective-permute-start(bf16[512,128]{1,0:T(8,128)(2,1)S(1)} %get-tuple-element.19), channel_id=1, source_target_pairs={{0,16},{16,0},{1,17},{17,1},{2,18},{18,2},{3,19},{19,3},{4,20},{20... | collective-permute-start | bytes 393224 | tf_op jit(solution)/shard_map/ppermute | solution.py:227
  49.5 10.6 %copy-start.7 = (bf16[512,512]{1,0:T(8,128)(2,1)S(1)}, bf16[512,512]{1,0:T(8,128)(2,1)}, u32[]{:S(2)}) copy-start(bf16[512,512]{1,0:T(8,128)(2,1)} %wo_ref.1) | copy-start | bytes 1572868
  50.7 7.5 %collective-permute-start.15 = (bf16[512,128]{1,0:T(8,128)(2,1)S(1)}, bf16[512,128]{1,0:T(8,128)(2,1)S(1)}, u32[]{:S(2)}, u32[]{:S(2)}) collective-permute-start(bf16[512,128]{1,0:T(8,128)(2,1)S(1)} %get-tuple-element.18), channel_id=1, source_target_pairs={{0,16},{16,0},{1,17},{17,1},{2,18},{18,2},{3,19},{19,3},{4,20},{20... | collective-permute-start | bytes 393224 | tf_op jit(solution)/shard_map/ppermute | solution.py:227
  52.3 7.9 %copy-start.3 = (bf16[512,512]{1,0:T(8,128)(2,1)S(1)}, bf16[512,512]{1,0:T(8,128)(2,1)}, u32[]{:S(2)}) copy-start(bf16[512,512]{1,0:T(8,128)(2,1)} %wg_ref.1) | copy-start | bytes 1572868
  52.3 7.9 %copy-start.4 = (bf16[512,512]{1,0:T(8,128)(2,1)S(1)}, bf16[512,512]{1,0:T(8,128)(2,1)}, u32[]{:S(2)}) copy-start(bf16[512,512]{1,0:T(8,128)(2,1)} %wq_ref.1) | copy-start | bytes 1572868
  52.3 7.9 %copy-start.5 = (bf16[512,512]{1,0:T(8,128)(2,1)S(1)}, bf16[512,512]{1,0:T(8,128)(2,1)}, u32[]{:S(2)}) copy-start(bf16[512,512]{1,0:T(8,128)(2,1)} %wk_ref.1) | copy-start | bytes 1572868
  52.3 7.9 %copy-start.6 = (bf16[512,512]{1,0:T(8,128)(2,1)S(1)}, bf16[512,512]{1,0:T(8,128)(2,1)}, u32[]{:S(2)}) copy-start(bf16[512,512]{1,0:T(8,128)(2,1)} %wv_ref.1) | copy-start | bytes 1572868
  53.5 6.7 %collective-permute-start.14 = (bf16[512,128]{1,0:T(8,128)(2,1)S(1)}, bf16[512,128]{1,0:T(8,128)(2,1)S(1)}, u32[]{:S(2)}, u32[]{:S(2)}) collective-permute-start(bf16[512,128]{1,0:T(8,128)(2,1)S(1)} %get-tuple-element.17), channel_id=1, source_target_pairs={{0,16},{16,0},{1,17},{17,1},{2,18},{18,2},{3,19},{19,3},{4,20},{20... | collective-permute-start | bytes 393224 | tf_op jit(solution)/shard_map/ppermute | solution.py:227
  (3 other events, 2.0 us)
